TPU v7x, 32 devices: a whole 2x2x4 slice. The times are simulated.
32 devices in a mesh: batch: 2 (over x), items: 16 (over z, y, core).
Axes of the slice: x: 2, y: 2, z: 4, core: 2. Of those that a mesh axis runs over, the one named last changes fastest.
Arguments:
- users: bfloat16 [1280, 256], P(('batch', 'items')), may hold values from -6 to 6
- items: bfloat16 [8192, 256], P(('batch', 'items')), may hold values from -6 to 6
- pos_ids: int32 [1280], P(('batch', 'items')), may hold values from 0 to 8191
Outputs:
- loss: float32 [1280], P(('batch', 'items'))
- user_grad: float32 [1280, 256], P(('batch', 'items'))
- item_grad: float32 [8192, 256], P(('batch', 'items'))
All inputs are finite; a program needn't handle non-finite values.
Results may differ from a plain program's by a relative error of at most 0.0015.
Values may be sent and summed in bfloat16 or wider, within the bound.
A program may use at most 64 MiB of HBM per device.

v0:
```python
import functools
import math

import jax
import jax.numpy as jnp
from jax import lax
from jax.experimental import pallas as pl
from jax.experimental.pallas import tpu as pltpu
from jax.sharding import PartitionSpec as P

F32 = jnp.float32
BF16 = jnp.bfloat16
MESH = pl.DeviceIdType.MESH
NT = (((1,), (1,)), ((), ()))
TN = (((0,), (0,)), ((), ()))
QUAD = 4
PARTS = 2


def kernel(
    peers, slots, users_ref, items_ref, pos_ref,
    loss_ref, ug_out, ig_out, x_recv,
    uall, pall, iall, ucat, e_ref, w_ref, top_ref, part_ref, lse_ref, stat, stat_all,
    term, ug_send, near_recv, far_recv, d_send, d_recv, x_send, ug_ref, ig_ref,
    u_ss, u_rs, p_ss, p_rs, i_ss, i_rs, s_ss, s_rs, g_ss, g_rs, d_ss, d_rs, x_ss, x_rs, in_sem, out_sem,
):
    own = users_ref.shape[0]
    per = items_ref.shape[0]
    chunks = peers // slots
    batch = lax.axis_index("batch")
    index = lax.axis_index("items")
    core = lax.rem(index, 2)
    me = index // 2
    twin = index + 1 - 2 * core
    other = 1 - batch
    total_index = 2 * peers

    def at(peer):
        return {"batch": batch, "items": 2 * peer + core}

    def peer_at(step):
        return lax.rem(me + step, peers)

    to_twin = {"batch": batch, "items": twin}
    to_other = {"batch": other, "items": index}

    def remote(src, dst, ss, rs, device):
        return pltpu.make_async_remote_copy(
            src_ref=src, dst_ref=dst, send_sem=ss, recv_sem=rs, device_id=device, device_id_type=MESH
        )

    barrier = pltpu.get_barrier_semaphore()

    def steps(count, first, body):
        if count <= 8:
            for step in range(count - 1, first - 1, -1):
                body(step)
        else:
            pl.loop(first, count)(body)

    def each(body):
        steps(peers, 1, body)

    def hello(step):
        pl.semaphore_signal(barrier, inc=1, device_id=at(peer_at(step)), device_id_type=MESH)

    mine_in = (
        pltpu.make_async_copy(items_ref, iall.at[0], in_sem.at[0]),
        pltpu.make_async_copy(users_ref, uall.at[me], in_sem.at[1]),
        pltpu.make_async_copy(pos_ref, pall.at[me], in_sem.at[2]),
    )
    each(hello)
    pl.semaphore_signal(barrier, inc=1, device_id=to_twin, device_id_type=MESH)
    pl.semaphore_signal(barrier, inc=1, device_id=to_other, device_id_type=MESH)
    for copy in mine_in:
        copy.start()
    for copy in mine_in:
        copy.wait()
    pl.semaphore_wait(barrier, peers + 1)

    def users_copy(step, source):
        return remote(uall.at[me], uall.at[source], u_ss.at[step], u_rs.at[source], at(peer_at(step)))

    def pos_copy(step, source):
        return remote(pall.at[me], pall.at[source], p_ss.at[step], p_rs.at[source], at(peer_at(step)))

    def stat_copy(step, source):
        return remote(stat, stat_all.at[source], s_ss.at[step], s_rs.at[source], at(peer_at(step)))

    half = peers // 2
    side = me // half
    place = lax.rem(me, half)

    def near_at(step):
        return side * half + lax.rem(place + step, half)

    def far_at(step):
        return (1 - side) * half + lax.rem(place + step, half)

    def near_copy(step, source):
        peer = near_at(step)
        return remote(term.at[peer], near_recv.at[source], g_ss.at[peer], g_rs.at[source], at(peer))

    def far_copy(step, source):
        peer = far_at(step)
        return remote(ug_send.at[peer], far_recv.at[source], g_ss.at[peer], g_rs.at[source], at(peer))

    def items_copy(src, slot, device):
        return remote(src, iall.at[slot], i_ss.at[slot], i_rs.at[slot], device)

    from_other = items_copy(iall.at[0], 2, to_other)
    from_twin = items_copy(iall.at[0], 1, to_twin)
    from_diag = items_copy(iall.at[2], 3, to_twin)
    from_other.start()
    each(lambda step: pos_copy(step, me).start())
    each(lambda step: users_copy(step, me).start())
    from_twin.start()
    from_other.wait_recv()
    from_diag.start()
    each(lambda step: users_copy(step, peer_at(step)).wait_recv())
    each(lambda step: pos_copy(step, peer_at(step)).wait_recv())

    def over_chunks(body):
        if chunks == 1:
            body(0)
        else:
            pl.loop(0, chunks)(body)

    homes = (
        batch * total_index + index,
        batch * total_index + twin,
        other * total_index + index,
        other * total_index + twin,
    )
    row = lax.broadcasted_iota(jnp.int32, (per, slots * own), 0)

    def ids_of(chunk):
        return jnp.concatenate([pall[chunk * slots + k] for k in range(slots)], axis=1)

    def prepare(chunk):
        ucat[chunk] = jnp.concatenate(
            [uall[chunk * slots + k].astype(F32) for k in range(slots)], axis=0
        ).astype(BF16)

    def forward(q, chunk):
        logit = lax.dot_general(iall[q], ucat[chunk], NT, preferred_element_type=F32)
        top = jnp.max(logit, axis=0, keepdims=True)
        hit = row == ids_of(chunk) - homes[q] * per
        e = jnp.exp(logit - top)
        e_ref[chunk, q] = e
        top_ref[chunk, q] = top
        part_ref[chunk, q, 0:1] = jnp.sum(e, axis=0, keepdims=True)
        part_ref[chunk, q, 1:2] = jnp.sum(jnp.where(hit, logit, 0.0), axis=0, keepdims=True)

    def summarize(chunk):
        tops = top_ref[chunk]
        top = jnp.max(tops, axis=0)
        total = jnp.sum(part_ref[chunk, :, 0:1] * jnp.exp(tops - top[None]), axis=0)
        stat[chunk, 0:1] = top + jnp.log(total)
        stat[chunk, 1:2] = jnp.sum(part_ref[chunk, :, 1:2], axis=0)

    over_chunks(prepare)
    over_chunks(functools.partial(forward, 0))
    from_twin.wait_recv()
    over_chunks(functools.partial(forward, 1))
    over_chunks(functools.partial(forward, 2))
    from_diag.wait_recv()
    over_chunks(functools.partial(forward, 3))
    over_chunks(summarize)
    each(lambda step: stat_copy(step, me).start())
    stat_all[me] = stat[...]
    each(lambda step: stat_copy(step, peer_at(step)).wait_recv())

    def rescale(chunk):
        parts = stat_all[:, chunk]
        lses = parts[:, 0:1]
        peak = jnp.max(lses, axis=0)
        lse = peak + jnp.log(jnp.sum(jnp.exp(lses - peak[None]), axis=0))
        lse_ref[chunk] = lse - jnp.sum(parts[:, 1:2], axis=0)
        top_ref[chunk] = jnp.exp(top_ref[chunk] - lse[None])

    def user_terms(chunk):
        grad = jnp.zeros((slots * own, ucat.shape[2]), F32)
        for q in range(QUAD):
            hit = row == ids_of(chunk) - homes[q] * per
            w = e_ref[chunk, q] * top_ref[chunk, q] - jnp.where(hit, 1.0, 0.0)
            w = w.astype(BF16)
            w_ref[chunk, q] = w
            grad = grad + lax.dot_general(w, iall[q], TN, preferred_element_type=F32)
        for k in range(slots):
            part = grad[k * own : (k + 1) * own]
            term[chunk * slots + k] = part
            ug_send[chunk * slots + k] = part.astype(BF16)

    rows = per // PARTS

    def item_term(q, p):
        def one(chunk):
            return jnp.dot(
                w_ref[chunk, q, p * rows : (p + 1) * rows], ucat[chunk], preferred_element_type=F32
            )

        if chunks == 1:
            return one(0)
        return lax.fori_loop(1, chunks, lambda chunk, acc: acc + one(chunk), one(0))

    def twin_copy(k, p):
        return remote(d_send.at[k, p], d_recv.at[k, p], d_ss.at[k, p], d_rs.at[k, p], to_twin)

    def across_copy(p):
        return remote(x_send.at[p], x_recv.at[p], x_ss.at[p], x_rs.at[p], to_other)

    over_chunks(rescale)
    over_chunks(user_terms)
    steps(half, 0, lambda step: far_copy(step, me).start())
    for p in range(PARTS):
        d_send[0, p] = item_term(3, p)
        twin_copy(0, p).start()
    steps(half, 1, lambda step: near_copy(step, me).start())
    for p in range(PARTS):
        far = item_term(2, p)
        twin_copy(0, p).wait_recv()
        x_send[p] = (far + d_recv[0, p]).astype(BF16)
        across_copy(p).start()
    for p in range(PARTS):
        d_send[1, p] = item_term(1, p)
        twin_copy(1, p).start()
    for p in range(PARTS):
        ig_ref[p * rows : (p + 1) * rows] = item_term(0, p)

    losses = lse_ref[me // slots]
    loss = jnp.zeros((1, own), F32)
    for k in range(slots):
        loss = jnp.where(lax.rem(me, slots) == k, losses[:, k * own : (k + 1) * own], loss)
    loss_ref[...] = loss

    for p in range(PARTS):
        twin_copy(1, p).wait_recv()
        ig_ref[p * rows : (p + 1) * rows] += d_recv[1, p]
    ig_copy = pltpu.make_async_copy(ig_ref, ig_out, out_sem.at[0])
    ig_copy.start()
    ug_ref[...] = term[me]

    def gather_near(step):
        near_copy(step, near_at(step)).wait_recv()
        ug_ref[...] += near_recv[near_at(step)]

    def gather_far(step):
        far_copy(step, far_at(step)).wait_recv()
        ug_ref[...] += far_recv[far_at(step)].astype(F32)

    steps(half, 1, gather_near)
    steps(half, 0, gather_far)
    ug_copy = pltpu.make_async_copy(ug_ref, ug_out, out_sem.at[1])
    ug_copy.start()
    for p in range(PARTS):
        across_copy(p).wait_recv()
    ig_copy.wait()
    ug_copy.wait()
    from_other.wait_send()
    from_twin.wait_send()
    from_diag.wait_send()
    for p in range(PARTS):
        twin_copy(0, p).wait_send()
        twin_copy(1, p).wait_send()
        across_copy(p).wait_send()
    for copy in (users_copy, pos_copy, stat_copy):
        each(lambda step: copy(step, me).wait_send())
    steps(half, 0, lambda step: far_copy(step, me).wait_send())
    steps(half, 1, lambda step: near_copy(step, me).wait_send())


def settle(loss_in, ug_in, ig_in, x_in, loss_ref, ug_ref, ig_ref):
    loss_ref[...] = loss_in[...]
    ug_ref[...] = ug_in[...]
    rows = x_in.shape[1]
    for p in range(PARTS):
        block = slice(p * rows, (p + 1) * rows)
        ig_ref[block] = ig_in[block] + x_in[p].astype(F32)


def local(users, items, pos_ids):
    own, width = users.shape
    per = items.shape[0]
    peers = lax.axis_size("items") // 2
    slots = math.gcd(peers, 8)
    chunks = peers // slots
    lanes = slots * own
    dma = pltpu.SemaphoreType.DMA
    vmem = pl.BlockSpec(memory_space=pltpu.VMEM)
    hbm = pl.BlockSpec(memory_space=pltpu.HBM)
    loss, user_grad, item_grad, far_terms = pl.pallas_call(
        functools.partial(kernel, peers, slots),
        out_shape=(
            jax.ShapeDtypeStruct((1, own), F32),
            jax.ShapeDtypeStruct((own, width), F32),
            jax.ShapeDtypeStruct((per, width), F32),
            jax.ShapeDtypeStruct((PARTS, per // PARTS, width), BF16),
        ),
        in_specs=[hbm] * 3,
        out_specs=(vmem, hbm, hbm, hbm),
        scratch_shapes=[
            pltpu.VMEM((peers, own, width), BF16),
            pltpu.VMEM((peers, 1, own), jnp.int32),
            pltpu.VMEM((QUAD, per, width), BF16),
            pltpu.VMEM((chunks, lanes, width), BF16),
            pltpu.VMEM((chunks, QUAD, per, lanes), F32),
            pltpu.VMEM((chunks, QUAD, per, lanes), BF16),
            pltpu.VMEM((chunks, QUAD, 1, lanes), F32),
            pltpu.VMEM((chunks, QUAD, 2, lanes), F32),
            pltpu.VMEM((chunks, 1, lanes), F32),
            pltpu.VMEM((chunks, 2, lanes), F32),
            pltpu.VMEM((peers, chunks, 2, lanes), F32),
            pltpu.VMEM((peers, own, width), F32),
            pltpu.VMEM((peers, own, width), BF16),
            pltpu.VMEM((peers, own, width), F32),
            pltpu.VMEM((peers, own, width), BF16),
            pltpu.VMEM((2, PARTS, per // PARTS, width), F32),
            pltpu.VMEM((2, PARTS, per // PARTS, width), F32),
            pltpu.VMEM((PARTS, per // PARTS, width), BF16),
            pltpu.VMEM((own, width), F32),
            pltpu.VMEM((per, width), F32),
            dma((peers,)), dma((peers,)),
            dma((peers,)), dma((peers,)),
            dma((QUAD,)), dma((QUAD,)),
            dma((peers,)), dma((peers,)),
            dma((peers,)), dma((peers,)),
            dma((2, PARTS)), dma((2, PARTS)),
            dma((PARTS,)), dma((PARTS,)),
            dma((3,)),
            dma((2,)),
        ],
        compiler_params=pltpu.CompilerParams(
            collective_id=0, has_side_effects=True, vmem_limit_bytes=60 * 1024 * 1024
        ),
    )(users, items, pos_ids.reshape(1, own))
    loss, user_grad, item_grad = pl.pallas_call(
        settle,
        out_shape=(
            jax.ShapeDtypeStruct((1, own), F32),
            jax.ShapeDtypeStruct((own, width), F32),
            jax.ShapeDtypeStruct((per, width), F32),
        ),
        in_specs=[vmem] * 4,
        out_specs=(vmem,) * 3,
    )(loss, user_grad, item_grad, far_terms)
    return loss.reshape(own), user_grad, item_grad


def solution(mesh):
    placed = (P(("batch", "items"), None), P(("batch", "items"), None), P(("batch", "items")))
    return jax.shard_map(
        local,
        mesh=mesh,
        in_specs=placed,
        out_specs=(P(("batch", "items")), P(("batch", "items"), None), P(("batch", "items"), None)),
        check_vma=False,
    )
```

profile of v0, /device:TPU:0, one launch (start us, length us, event | category | flops | bytes accessed | tf_op | source)
XLA Modules:
  0.0 26.7 jit_solution(265417087796027730)
XLA Ops:
  0.6 24.3 %shard_map.58 = (f32[1,40]{1,0:T(1,128)}, f32[40,256]{1,0:T(8,128)}, f32[256,256]{1,0:T(8,128)}, bf16[2,128,256]{2,1,0:T(8,128)(2,1)}) custom-call(bf16[40,256]{1,0:T(8,128)(2,1)} %users_ref.1, bf16[256,256]{1,0:T(8,128)(2,1)} %items_ref.1, s32[1,40]{1,0:T(1,128)} %bitcast.2), custom_call_target="tpu_custom_call" | custom-call | tf_op jit(solution)/shard_map/pallas_call | solution.py:292
  24.9 1.7 %shard_map.59 = (f32[1,40]{1,0:T(1,128)}, f32[40,256]{1,0:T(8,128)}, f32[256,256]{1,0:T(8,128)}) custom-call(f32[1,40]{1,0:T(1,128)} %get-tuple-element.10.loss_in, f32[40,256]{1,0:T(8,128)} %get-tuple-element.11.ug_in, f32[256,256]{1,0:T(8,128)} %get-tuple-element.12.ig_in, bf16[2,128,256]{2,1,0:T(8,128)(2,1)} %get-tuple-element.13.x_in), custom_call_target="tpu_custom_call" | custom-call | tf_op jit(solution)/shard_map/pallas_call | solution.py:337
where the time goes:
time: 26.8 us; the launch traced here: 26.7 us
  Pallas kernels  26 us (97%)
  between operations  0.64 us (2%)
    pallas_call x1, Pallas kernels, local(): pl.pallas_call(functools.partial(kernel, peers, slots), out_shape=(jax.Sh...  24.3 us
    pallas_call x1, Pallas kernels, local(): pl.pallas_call(settle, out_shape=(jax.ShapeDtypeStruct((1, own), F32), ja...  1.74 us

commit v1 on v0

--- a/solution.py
+++ b/solution.py
@@ -19,10 +19,10 @@
 
 def kernel(
     peers, slots, users_ref, items_ref, pos_ref,
-    loss_ref, ug_out, ig_out, x_recv,
+    loss_ref, ug_ref, ig_ref, x_recv,
     uall, pall, iall, ucat, e_ref, w_ref, top_ref, part_ref, lse_ref, stat, stat_all,
-    term, ug_send, near_recv, far_recv, d_send, d_recv, x_send, ug_ref, ig_ref,
-    u_ss, u_rs, p_ss, p_rs, i_ss, i_rs, s_ss, s_rs, g_ss, g_rs, d_ss, d_rs, x_ss, x_rs, in_sem, out_sem,
+    term, ug_send, near_recv, far_recv, d_send, d_recv, x_send,
+    u_ss, u_rs, p_ss, p_rs, i_ss, i_rs, s_ss, s_rs, g_ss, g_rs, d_ss, d_rs, x_ss, x_rs, in_sem,
 ):
     own = users_ref.shape[0]
     per = items_ref.shape[0]
@@ -237,8 +237,6 @@
     for p in range(PARTS):
         twin_copy(1, p).wait_recv()
         ig_ref[p * rows : (p + 1) * rows] += d_recv[1, p]
-    ig_copy = pltpu.make_async_copy(ig_ref, ig_out, out_sem.at[0])
-    ig_copy.start()
     ug_ref[...] = term[me]
 
     def gather_near(step):
@@ -251,12 +249,8 @@
 
     steps(half, 1, gather_near)
     steps(half, 0, gather_far)
-    ug_copy = pltpu.make_async_copy(ug_ref, ug_out, out_sem.at[1])
-    ug_copy.start()
     for p in range(PARTS):
         across_copy(p).wait_recv()
-    ig_copy.wait()
-    ug_copy.wait()
     from_other.wait_send()
     from_twin.wait_send()
     from_diag.wait_send()
@@ -292,13 +286,13 @@
     loss, user_grad, item_grad, far_terms = pl.pallas_call(
         functools.partial(kernel, peers, slots),
         out_shape=(
-            jax.ShapeDtypeStruct((1, own), F32),
-            jax.ShapeDtypeStruct((own, width), F32),
-            jax.ShapeDtypeStruct((per, width), F32),
-            jax.ShapeDtypeStruct((PARTS, per // PARTS, width), BF16),
+            pltpu.VMEM((1, own), F32),
+            pltpu.VMEM((own, width), F32),
+            pltpu.VMEM((per, width), F32),
+            pltpu.VMEM((PARTS, per // PARTS, width), BF16),
         ),
         in_specs=[hbm] * 3,
-        out_specs=(vmem, hbm, hbm, hbm),
+        out_specs=(vmem, vmem, vmem, vmem),
         scratch_shapes=[
             pltpu.VMEM((peers, own, width), BF16),
             pltpu.VMEM((peers, 1, own), jnp.int32),
@@ -318,8 +312,6 @@
             pltpu.VMEM((2, PARTS, per // PARTS, width), F32),
             pltpu.VMEM((2, PARTS, per // PARTS, width), F32),
             pltpu.VMEM((PARTS, per // PARTS, width), BF16),
-            pltpu.VMEM((own, width), F32),
-            pltpu.VMEM((per, width), F32),
             dma((peers,)), dma((peers,)),
             dma((peers,)), dma((peers,)),
             dma((QUAD,)), dma((QUAD,)),
@@ -328,12 +320,11 @@
             dma((2, PARTS)), dma((2, PARTS)),
             dma((PARTS,)), dma((PARTS,)),
             dma((3,)),
-            dma((2,)),
         ],
         compiler_params=pltpu.CompilerParams(
-            collective_id=0, has_side_effects=True, vmem_limit_bytes=60 * 1024 * 1024
+            collective_id=0, has_side_effects=True, vmem_limit_bytes=32 * 1024 * 1024
         ),
-    )(users, items, pos_ids.reshape(1, own))
+    )(*(pltpu.with_memory_space_constraint(v, pltpu.HBM) for v in (users, items, pos_ids.reshape(1, own))))
     loss, user_grad, item_grad = pl.pallas_call(
         settle,
         out_shape=(
@@ -343,6 +334,7 @@
         ),
         in_specs=[vmem] * 4,
         out_specs=(vmem,) * 3,
+        compiler_params=pltpu.CompilerParams(vmem_limit_bytes=4 * 1024 * 1024),
     )(loss, user_grad, item_grad, far_terms)
     return loss.reshape(own), user_grad, item_grad
 

time: 26.8 us -> 25.1 us (0.937)
  Pallas kernels: 26 us -> 24.3 us
    pallas_call x1, Pallas kernels: 1.74 us -> 0.74 us  [local(): pl.pallas_call(settle, out_shape=(jax.ShapeDtypeStruct((1, own), F32), ja...]
    pallas_call x1, Pallas kernels: 24.3 us -> 23.5 us  [local(): pl.pallas_call(functools.partial(kernel, peers, slots), out_shape=(pltpu....]
where the time goes in v1:
time: 25.1 us; the launch traced here: 24.9 us
  Pallas kernels  24.3 us (97%)
  between operations  0.64 us (3%)
    pallas_call x1, Pallas kernels, local(): pl.pallas_call(functools.partial(kernel, peers, slots), out_shape=(pltpu....  23.5 us
    pallas_call x1, Pallas kernels, local(): pl.pallas_call(settle, out_shape=(jax.ShapeDtypeStruct((1, own), F32), ja...  0.74 us

profile of v1, /device:TPU:0, one launch (start us, length us, event | category | flops | bytes accessed | tf_op | source)
XLA Modules:
  0.0 24.9 jit_solution(18152897761881621187)
XLA Ops:
  0.6 23.5 %shard_map.58 = (f32[1,40]{1,0:T(1,128)S(1)}, f32[40,256]{1,0:T(8,128)S(1)}, f32[256,256]{1,0:T(8,128)S(1)}, bf16[2,128,256]{2,1,0:T(8,128)(2,1)S(1)}) custom-call(bf16[40,256]{1,0:T(8,128)(2,1)} %users_ref.1, bf16[256,256]{1,0:T(8,128)(2,1)} %items_ref.1, s32[1,40]{1,0:T(1,128)} %bitcast.2), custom_call_target="tpu_custom_call" | custom-call | tf_op jit(solution)/shard_map/pallas_call | solution.py:286
  24.2 0.7 %shard_map.59 = (f32[1,40]{1,0:T(1,128)}, f32[40,256]{1,0:T(8,128)}, f32[256,256]{1,0:T(8,128)}) custom-call(f32[1,40]{1,0:T(1,128)S(1)} %get-tuple-element.10.loss_in, f32[40,256]{1,0:T(8,128)S(1)} %get-tuple-element.11.ug_in, f32[256,256]{1,0:T(8,128)S(1)} %get-tuple-element.12.ig_in, bf16[2,128,256]{2,1,0:T(8,128)(2,1)S(1)} %get-tuple-element.13.x_in), custom_call_target="tpu_custom_call" | custom-call | tf_op jit(solution)/shard_map/pallas_call | solution.py:328

commit v2 on v1

--- a/solution.py
+++ b/solution.py
@@ -19,10 +19,11 @@
 
 def kernel(
     peers, slots, users_ref, items_ref, pos_ref,
-    loss_ref, ug_ref, ig_ref, x_recv,
-    uall, pall, iall, ucat, e_ref, w_ref, top_ref, part_ref, lse_ref, stat, stat_all,
-    term, ug_send, near_recv, far_recv, d_send, d_recv, x_send,
-    u_ss, u_rs, p_ss, p_rs, i_ss, i_rs, s_ss, s_rs, g_ss, g_rs, d_ss, d_rs, x_ss, x_rs, in_sem,
+    loss_ref, ug_ref, ig_ref,
+    uall, pall, iall, ucat, e_ref, w_ref, top_ref, part_ref, loss_all, stat, stat_all,
+    term, ug_send, near_recv, far_recv, mates, mate_ids, mate_cat, mate_logit, lse_ref, mate_lse,
+    u_ss, u_rs, p_ss, p_rs, i_ss, i_rs, s_ss, s_rs, g_ss, g_rs, m_ss, m_rs, n_ss, n_rs, l_ss, l_rs,
+    in_sem, ready, x_ready,
 ):
     own = users_ref.shape[0]
     per = items_ref.shape[0]
@@ -43,6 +44,7 @@
 
     to_twin = {"batch": batch, "items": twin}
     to_other = {"batch": other, "items": index}
+    to_diag = {"batch": other, "items": twin}
 
     def remote(src, dst, ss, rs, device):
         return pltpu.make_async_remote_copy(
@@ -61,22 +63,50 @@
     def each(body):
         steps(peers, 1, body)
 
-    def hello(step):
-        pl.semaphore_signal(barrier, inc=1, device_id=at(peer_at(step)), device_id_type=MESH)
+    def rising(body):
+        if peers <= 8:
+            for step in range(1, peers):
+                body(step)
+        else:
+            pl.loop(1, peers)(body)
+
+    def greet(step):
+        peer = peer_at(step)
+
+        @pl.when(peer > me)
+        def _():
+            pl.semaphore_signal(barrier, inc=1, device_id=at(peer), device_id_type=MESH)
+
+    def answer(step):
+        peer = peer_at(step)
+
+        @pl.when(peer < me)
+        def _():
+            pl.semaphore_signal(ready.at[me], inc=1, device_id=at(peer), device_id_type=MESH)
 
     mine_in = (
         pltpu.make_async_copy(items_ref, iall.at[0], in_sem.at[0]),
         pltpu.make_async_copy(users_ref, uall.at[me], in_sem.at[1]),
         pltpu.make_async_copy(pos_ref, pall.at[me], in_sem.at[2]),
     )
-    each(hello)
+    each(greet)
     pl.semaphore_signal(barrier, inc=1, device_id=to_twin, device_id_type=MESH)
-    pl.semaphore_signal(barrier, inc=1, device_id=to_other, device_id_type=MESH)
+
+    @pl.when(batch == 0)
+    def _():
+        pl.semaphore_signal(barrier, inc=1, device_id=to_other, device_id_type=MESH)
+
     for copy in mine_in:
         copy.start()
+    pl.semaphore_wait(barrier, me + batch + 1)
+    each(answer)
+
+    @pl.when(batch == 1)
+    def _():
+        pl.semaphore_signal(x_ready.at[0], inc=1, device_id=to_other, device_id_type=MESH)
+
     for copy in mine_in:
         copy.wait()
-    pl.semaphore_wait(barrier, peers + 1)
 
     def users_copy(step, source):
         return remote(uall.at[me], uall.at[source], u_ss.at[step], u_rs.at[source], at(peer_at(step)))
@@ -105,20 +135,85 @@
         peer = far_at(step)
         return remote(ug_send.at[peer], far_recv.at[source], g_ss.at[peer], g_rs.at[source], at(peer))
 
-    def items_copy(src, slot, device):
-        return remote(src, iall.at[slot], i_ss.at[slot], i_rs.at[slot], device)
-
-    from_other = items_copy(iall.at[0], 2, to_other)
-    from_twin = items_copy(iall.at[0], 1, to_twin)
-    from_diag = items_copy(iall.at[2], 3, to_twin)
-    from_other.start()
-    each(lambda step: pos_copy(step, me).start())
-    each(lambda step: users_copy(step, me).start())
-    from_twin.start()
-    from_other.wait_recv()
-    from_diag.start()
-    each(lambda step: users_copy(step, peer_at(step)).wait_recv())
-    each(lambda step: pos_copy(step, peer_at(step)).wait_recv())
+    half_rows = per // PARTS
+
+    def items_copy(source, slot, p, device):
+        block = pl.ds(p * half_rows, half_rows)
+        return remote(
+            iall.at[source, block], iall.at[slot, block], i_ss.at[slot, p], i_rs.at[slot, p], device
+        )
+
+    from_other = [items_copy(0, 2, p, to_other) for p in range(PARTS)]
+    from_twin = [items_copy(0, 1, p, to_twin) for p in range(PARTS)]
+    from_diag = [items_copy(2, 3, p, to_twin) for p in range(PARTS)]
+
+    def send_down(step):
+        @pl.when(peer_at(step) < me)
+        def _():
+            pos_copy(step, me).start()
+            users_copy(step, me).start()
+
+    def send_up(step):
+        peer = peer_at(step)
+
+        @pl.when(peer > me)
+        def _():
+            pl.semaphore_wait(ready.at[peer], 1)
+            pos_copy(step, me).start()
+            users_copy(step, me).start()
+
+    @pl.when(batch == 1)
+    def _():
+        for copy in from_other:
+            copy.start()
+
+    each(send_down)
+    for copy in from_twin:
+        copy.start()
+
+    @pl.when(batch == 0)
+    def _():
+        pl.semaphore_wait(x_ready.at[0], 1)
+        for copy in from_other:
+            copy.start()
+
+    rising(send_up)
+    for p in range(PARTS):
+        from_other[p].wait_recv()
+        from_diag[p].start()
+    def near_in(step):
+        source = near_at(step)
+        users_copy(step, source).wait_recv()
+        pos_copy(step, source).wait_recv()
+
+    def far_in(step):
+        source = far_at(step)
+        users_copy(step, source).wait_recv()
+        pos_copy(step, source).wait_recv()
+
+    def mate_copy(src, ids, k, p, part, device):
+        block = pl.ds(part * half, half)
+        return (
+            remote(ids.at[block], mate_ids.at[k, block], n_ss.at[k, p], n_rs.at[k, p], device),
+            remote(src.at[block], mates.at[k, block], m_ss.at[k, p], m_rs.at[k, p], device),
+        )
+
+    halves = (side, 1 - side)
+    to_mates = [
+        [mate_copy(uall, pall, 1, p, halves[p], to_other) for p in range(2)],
+        [mate_copy(uall, pall, 0, p, halves[p], to_twin) for p in range(2)],
+    ]
+    onward = [mate_copy(mates.at[1], mate_ids.at[1], 2, p, halves[p], to_twin) for p in range(2)]
+
+    def lend(p):
+        for pair in to_mates:
+            for copy in pair[p]:
+                copy.start()
+
+    steps(half, 1, near_in)
+    lend(0)
+    steps(half, 0, far_in)
+    lend(1)
 
     def over_chunks(body):
         if chunks == 1:
@@ -134,13 +229,25 @@
     )
     row = lax.broadcasted_iota(jnp.int32, (per, slots * own), 0)
 
+    def lane_ids(ids, chunk):
+        return jnp.concatenate([ids[chunk * slots + k] for k in range(slots)], axis=1)
+
     def ids_of(chunk):
-        return jnp.concatenate([pall[chunk * slots + k] for k in range(slots)], axis=1)
+        return lane_ids(pall, chunk)
+
+    def joined(blocks, chunk):
+        return jnp.concatenate(
+            [blocks[chunk * slots + k].astype(F32) for k in range(slots)], axis=0
+        ).astype(BF16)
 
     def prepare(chunk):
-        ucat[chunk] = jnp.concatenate(
-            [uall[chunk * slots + k].astype(F32) for k in range(slots)], axis=0
-        ).astype(BF16)
+        ucat[chunk] = joined(uall, chunk)
+
+    def meet(k, chunk):
+        mate_cat[k, chunk] = joined(mates.at[k], chunk)
+        mate_logit[k, chunk] = lax.dot_general(
+            iall[0], mate_cat[k, chunk], NT, preferred_element_type=F32
+        )
 
     def forward(q, chunk):
         logit = lax.dot_general(iall[q], ucat[chunk], NT, preferred_element_type=F32)
@@ -161,14 +268,29 @@
 
     over_chunks(prepare)
     over_chunks(functools.partial(forward, 0))
-    from_twin.wait_recv()
+    for copy in from_twin:
+        copy.wait_recv()
     over_chunks(functools.partial(forward, 1))
     over_chunks(functools.partial(forward, 2))
-    from_diag.wait_recv()
+    for copy in from_diag:
+        copy.wait_recv()
     over_chunks(functools.partial(forward, 3))
     over_chunks(summarize)
     each(lambda step: stat_copy(step, me).start())
     stat_all[me] = stat[...]
+
+    def mate_in(k, p):
+        for copy in mate_copy(uall, pall, k, p, halves[p], to_twin):
+            copy.wait_recv()
+
+    for p in range(2):
+        mate_in(0, p)
+    over_chunks(functools.partial(meet, 0))
+    for p in range(2):
+        mate_in(1, p)
+        for copy in onward[p]:
+            copy.start()
+    over_chunks(functools.partial(meet, 1))
     each(lambda step: stat_copy(step, peer_at(step)).wait_recv())
 
     def rescale(chunk):
@@ -176,7 +298,8 @@
         lses = parts[:, 0:1]
         peak = jnp.max(lses, axis=0)
         lse = peak + jnp.log(jnp.sum(jnp.exp(lses - peak[None]), axis=0))
-        lse_ref[chunk] = lse - jnp.sum(parts[:, 1:2], axis=0)
+        lse_ref[chunk] = lse
+        loss_all[chunk] = lse - jnp.sum(parts[:, 1:2], axis=0)
         top_ref[chunk] = jnp.exp(top_ref[chunk] - lse[None])
 
     def user_terms(chunk):
@@ -192,51 +315,44 @@
             term[chunk * slots + k] = part
             ug_send[chunk * slots + k] = part.astype(BF16)
 
-    rows = per // PARTS
-
-    def item_term(q, p):
-        def one(chunk):
-            return jnp.dot(
-                w_ref[chunk, q, p * rows : (p + 1) * rows], ucat[chunk], preferred_element_type=F32
-            )
-
+    def own_term(chunk):
+        return jnp.dot(w_ref[chunk, 0], ucat[chunk], preferred_element_type=F32)
+
+    def mate_term(k, chunk):
+        hit = row == lane_ids(mate_ids.at[k], chunk) - homes[0] * per
+        w = jnp.exp(mate_logit[k, chunk] - mate_lse[k, chunk]) - jnp.where(hit, 1.0, 0.0)
+        return jnp.dot(w.astype(BF16), mate_cat[k, chunk], preferred_element_type=F32)
+
+    def total_of(one):
         if chunks == 1:
             return one(0)
         return lax.fori_loop(1, chunks, lambda chunk, acc: acc + one(chunk), one(0))
 
-    def twin_copy(k, p):
-        return remote(d_send.at[k, p], d_recv.at[k, p], d_ss.at[k, p], d_rs.at[k, p], to_twin)
-
-    def across_copy(p):
-        return remote(x_send.at[p], x_recv.at[p], x_ss.at[p], x_rs.at[p], to_other)
+    lse_copies = [
+        remote(lse_ref, mate_lse.at[k], l_ss.at[k], l_rs.at[k], device)
+        for k, device in enumerate((to_twin, to_other, to_diag))
+    ]
 
     over_chunks(rescale)
+    for copy in (lse_copies[1], lse_copies[2], lse_copies[0]):
+        copy.start()
     over_chunks(user_terms)
     steps(half, 0, lambda step: far_copy(step, me).start())
-    for p in range(PARTS):
-        d_send[0, p] = item_term(3, p)
-        twin_copy(0, p).start()
     steps(half, 1, lambda step: near_copy(step, me).start())
-    for p in range(PARTS):
-        far = item_term(2, p)
-        twin_copy(0, p).wait_recv()
-        x_send[p] = (far + d_recv[0, p]).astype(BF16)
-        across_copy(p).start()
-    for p in range(PARTS):
-        d_send[1, p] = item_term(1, p)
-        twin_copy(1, p).start()
-    for p in range(PARTS):
-        ig_ref[p * rows : (p + 1) * rows] = item_term(0, p)
-
-    losses = lse_ref[me // slots]
+    ig_ref[...] = total_of(own_term)
+    for p in range(2):
+        mate_in(2, p)
+    over_chunks(functools.partial(meet, 2))
+    for k in range(3):
+        lse_copies[k].wait_recv()
+        ig_ref[...] += total_of(functools.partial(mate_term, k))
+
+    losses = loss_all[me // slots]
     loss = jnp.zeros((1, own), F32)
     for k in range(slots):
         loss = jnp.where(lax.rem(me, slots) == k, losses[:, k * own : (k + 1) * own], loss)
     loss_ref[...] = loss
 
-    for p in range(PARTS):
-        twin_copy(1, p).wait_recv()
-        ig_ref[p * rows : (p + 1) * rows] += d_recv[1, p]
     ug_ref[...] = term[me]
 
     def gather_near(step):
@@ -249,28 +365,28 @@
 
     steps(half, 1, gather_near)
     steps(half, 0, gather_far)
-    for p in range(PARTS):
-        across_copy(p).wait_recv()
-    from_other.wait_send()
-    from_twin.wait_send()
-    from_diag.wait_send()
-    for p in range(PARTS):
-        twin_copy(0, p).wait_send()
-        twin_copy(1, p).wait_send()
-        across_copy(p).wait_send()
+    for copy in from_other + from_twin + from_diag:
+        copy.wait_send()
+    for p in range(2):
+        for copy in (*to_mates[0][p], *to_mates[1][p], *onward[p]):
+            copy.wait_send()
+    for copy in lse_copies:
+        copy.wait_send()
     for copy in (users_copy, pos_copy, stat_copy):
         each(lambda step: copy(step, me).wait_send())
     steps(half, 0, lambda step: far_copy(step, me).wait_send())
     steps(half, 1, lambda step: near_copy(step, me).wait_send())
 
 
-def settle(loss_in, ug_in, ig_in, x_in, loss_ref, ug_ref, ig_ref):
-    loss_ref[...] = loss_in[...]
-    ug_ref[...] = ug_in[...]
-    rows = x_in.shape[1]
-    for p in range(PARTS):
-        block = slice(p * rows, (p + 1) * rows)
-        ig_ref[block] = ig_in[block] + x_in[p].astype(F32)
+def settle(loss_in, ug_in, ig_in, loss_out, ug_out, ig_out, sems):
+    copies = [
+        pltpu.make_async_copy(src, dst, sems.at[k])
+        for k, (src, dst) in enumerate(((ig_in, ig_out), (ug_in, ug_out), (loss_in, loss_out)))
+    ]
+    for copy in copies:
+        copy.start()
+    for copy in copies:
+        copy.wait()
 
 
 def local(users, items, pos_ids):
@@ -283,16 +399,15 @@
     dma = pltpu.SemaphoreType.DMA
     vmem = pl.BlockSpec(memory_space=pltpu.VMEM)
     hbm = pl.BlockSpec(memory_space=pltpu.HBM)
-    loss, user_grad, item_grad, far_terms = pl.pallas_call(
+    loss, user_grad, item_grad = pl.pallas_call(
         functools.partial(kernel, peers, slots),
         out_shape=(
             pltpu.VMEM((1, own), F32),
             pltpu.VMEM((own, width), F32),
             pltpu.VMEM((per, width), F32),
-            pltpu.VMEM((PARTS, per // PARTS, width), BF16),
         ),
         in_specs=[hbm] * 3,
-        out_specs=(vmem, vmem, vmem, vmem),
+        out_specs=(vmem, vmem, vmem),
         scratch_shapes=[
             pltpu.VMEM((peers, own, width), BF16),
             pltpu.VMEM((peers, 1, own), jnp.int32),
@@ -309,20 +424,26 @@
             pltpu.VMEM((peers, own, width), BF16),
             pltpu.VMEM((peers, own, width), F32),
             pltpu.VMEM((peers, own, width), BF16),
-            pltpu.VMEM((2, PARTS, per // PARTS, width), F32),
-            pltpu.VMEM((2, PARTS, per // PARTS, width), F32),
-            pltpu.VMEM((PARTS, per // PARTS, width), BF16),
+            pltpu.VMEM((3, peers, own, width), BF16),
+            pltpu.VMEM((3, peers, 1, own), jnp.int32),
+            pltpu.VMEM((3, chunks, lanes, width), BF16),
+            pltpu.VMEM((3, chunks, per, lanes), F32),
+            pltpu.VMEM((chunks, 1, lanes), F32),
+            pltpu.VMEM((3, chunks, 1, lanes), F32),
             dma((peers,)), dma((peers,)),
             dma((peers,)), dma((peers,)),
-            dma((QUAD,)), dma((QUAD,)),
+            dma((QUAD, PARTS)), dma((QUAD, PARTS)),
             dma((peers,)), dma((peers,)),
             dma((peers,)), dma((peers,)),
-            dma((2, PARTS)), dma((2, PARTS)),
-            dma((PARTS,)), dma((PARTS,)),
+            dma((3, 2)), dma((3, 2)),
+            dma((3, 2)), dma((3, 2)),
+            dma((3,)), dma((3,)),
             dma((3,)),
+            pltpu.SemaphoreType.REGULAR((peers,)),
+            pltpu.SemaphoreType.REGULAR((1,)),
         ],
         compiler_params=pltpu.CompilerParams(
-            collective_id=0, has_side_effects=True, vmem_limit_bytes=32 * 1024 * 1024
+            collective_id=0, has_side_effects=True, vmem_limit_bytes=48 * 1024 * 1024
         ),
     )(*(pltpu.with_memory_space_constraint(v, pltpu.HBM) for v in (users, items, pos_ids.reshape(1, own))))
     loss, user_grad, item_grad = pl.pallas_call(
@@ -332,10 +453,11 @@
             jax.ShapeDtypeStruct((own, width), F32),
             jax.ShapeDtypeStruct((per, width), F32),
         ),
-        in_specs=[vmem] * 4,
-        out_specs=(vmem,) * 3,
+        in_specs=[vmem] * 3,
+        out_specs=(hbm,) * 3,
+        scratch_shapes=[dma((3,))],
         compiler_params=pltpu.CompilerParams(vmem_limit_bytes=4 * 1024 * 1024),
-    )(loss, user_grad, item_grad, far_terms)
+    )(loss, user_grad, item_grad)
     return loss.reshape(own), user_grad, item_grad
 
 

time: 25.1 us -> 24.3 us (0.968)
  Pallas kernels: 24.3 us -> 23.5 us
    pallas_call x1, Pallas kernels: 23.5 us -> 22.7 us  [local(): pl.pallas_call(functools.partial(kernel, peers, slots), out_shape=(pltpu....]
where the time goes in v2:
time: 24.3 us; the launch traced here: 24.1 us
  Pallas kernels  23.5 us (97%)
  between operations  0.64 us (3%)
    pallas_call x1, Pallas kernels, local(): pl.pallas_call(functools.partial(kernel, peers, slots), out_shape=(pltpu....  22.7 us
    pallas_call x1, Pallas kernels, local(): pl.pallas_call(settle, out_shape=(jax.ShapeDtypeStruct((1, own), F32), ja...  0.73 us

profile of v2, /device:TPU:0, one launch (start us, length us, event | category | flops | bytes accessed | tf_op | source)
XLA Modules:
  0.0 24.1 jit_solution(6523706329438940338)
XLA Ops:
  0.6 22.7 %shard_map.58 = (f32[1,40]{1,0:T(1,128)S(1)}, f32[40,256]{1,0:T(8,128)S(1)}, f32[256,256]{1,0:T(8,128)S(1)}) custom-call(bf16[40,256]{1,0:T(8,128)(2,1)} %users_ref.1, bf16[256,256]{1,0:T(8,128)(2,1)} %items_ref.1, s32[1,40]{1,0:T(1,128)} %bitcast.2), custom_call_target="tpu_custom_call" | custom-call | tf_op jit(solution)/shard_map/pallas_call | solution.py:402
  23.4 0.7 %shard_map.59 = (f32[1,40]{1,0:T(1,128)}, f32[40,256]{1,0:T(8,128)}, f32[256,256]{1,0:T(8,128)}) custom-call(f32[1,40]{1,0:T(1,128)S(1)} %get-tuple-element.9.loss_in, f32[40,256]{1,0:T(8,128)S(1)} %get-tuple-element.10.ug_in, f32[256,256]{1,0:T(8,128)S(1)} %get-tuple-element.11.ig_in), custom_call_target="tpu_custom_call" | custom-call | tf_op jit(solution)/shard_map/pallas_call | solution.py:449

commit v3 on v2

--- a/solution.py
+++ b/solution.py
@@ -20,7 +20,7 @@
 def kernel(
     peers, slots, users_ref, items_ref, pos_ref,
     loss_ref, ug_ref, ig_ref,
-    uall, pall, iall, ucat, e_ref, w_ref, top_ref, part_ref, loss_all, stat, stat_all,
+    uall, pall, iall, ucat, e_ref, logit_ref, blend, picked, top_ref, part_ref, loss_all, stat, stat_all,
     term, ug_send, near_recv, far_recv, mates, mate_ids, mate_cat, mate_logit, lse_ref, mate_lse,
     u_ss, u_rs, p_ss, p_rs, i_ss, i_rs, s_ss, s_rs, g_ss, g_rs, m_ss, m_rs, n_ss, n_rs, l_ss, l_rs,
     in_sem, ready, x_ready,
@@ -128,11 +128,15 @@
         return (1 - side) * half + lax.rem(place + step, half)
 
     def near_copy(step, source):
-        peer = near_at(step)
+        return to_near(near_at(step), source)
+
+    def far_copy(step, source):
+        return to_far(far_at(step), source)
+
+    def to_near(peer, source):
         return remote(term.at[peer], near_recv.at[source], g_ss.at[peer], g_rs.at[source], at(peer))
 
-    def far_copy(step, source):
-        peer = far_at(step)
+    def to_far(peer, source):
         return remote(ug_send.at[peer], far_recv.at[source], g_ss.at[peer], g_rs.at[source], at(peer))
 
     half_rows = per // PARTS
@@ -254,7 +258,9 @@
         top = jnp.max(logit, axis=0, keepdims=True)
         hit = row == ids_of(chunk) - homes[q] * per
         e = jnp.exp(logit - top)
-        e_ref[chunk, q] = e
+        e_ref[chunk, q] = e.astype(BF16)
+        if q == 0:
+            logit_ref[chunk] = logit
         top_ref[chunk, q] = top
         part_ref[chunk, q, 0:1] = jnp.sum(e, axis=0, keepdims=True)
         part_ref[chunk, q, 1:2] = jnp.sum(jnp.where(hit, logit, 0.0), axis=0, keepdims=True)
@@ -283,6 +289,24 @@
         for copy in mate_copy(uall, pall, k, p, halves[p], to_twin):
             copy.wait_recv()
 
+    def columns(rows):
+        return jnp.transpose(jnp.concatenate([rows] * (8 // rows.shape[0]), axis=0))
+
+    def gather_terms(chunk):
+        share = columns(
+            jnp.concatenate([top_ref[chunk, q] - stat[chunk, 0:1] for q in range(QUAD)], axis=0)
+        )
+        mix = jnp.zeros((slots * own, ucat.shape[2]), F32)
+        pick = jnp.zeros((slots * own, ucat.shape[2]), F32)
+        for q in range(QUAD):
+            hit = jnp.where(row == ids_of(chunk) - homes[q] * per, 1.0, 0.0).astype(BF16)
+            part = lax.dot_general(e_ref[chunk, q], iall[q], TN, preferred_element_type=F32)
+            mix = mix + part * jnp.exp(share[:, q : q + 1])
+            pick = pick + lax.dot_general(hit, iall[q], TN, preferred_element_type=F32)
+        blend[chunk] = mix
+        picked[chunk] = pick
+
+    over_chunks(gather_terms)
     for p in range(2):
         mate_in(0, p)
     over_chunks(functools.partial(meet, 0))
@@ -291,7 +315,12 @@
         for copy in onward[p]:
             copy.start()
     over_chunks(functools.partial(meet, 1))
+    for copy in from_other + from_twin + from_diag:
+        copy.wait_send()
+    for copy in (users_copy, pos_copy):
+        each(lambda step: copy(step, me).wait_send())
     each(lambda step: stat_copy(step, peer_at(step)).wait_recv())
+
 
     def rescale(chunk):
         parts = stat_all[:, chunk]
@@ -300,23 +329,19 @@
         lse = peak + jnp.log(jnp.sum(jnp.exp(lses - peak[None]), axis=0))
         lse_ref[chunk] = lse
         loss_all[chunk] = lse - jnp.sum(parts[:, 1:2], axis=0)
-        top_ref[chunk] = jnp.exp(top_ref[chunk] - lse[None])
 
     def user_terms(chunk):
-        grad = jnp.zeros((slots * own, ucat.shape[2]), F32)
-        for q in range(QUAD):
-            hit = row == ids_of(chunk) - homes[q] * per
-            w = e_ref[chunk, q] * top_ref[chunk, q] - jnp.where(hit, 1.0, 0.0)
-            w = w.astype(BF16)
-            w_ref[chunk, q] = w
-            grad = grad + lax.dot_general(w, iall[q], TN, preferred_element_type=F32)
+        share = columns(stat[chunk, 0:1] - lse_ref[chunk])[:, 0:1]
+        grad = blend[chunk] * jnp.exp(share) - picked[chunk]
         for k in range(slots):
             part = grad[k * own : (k + 1) * own]
             term[chunk * slots + k] = part
             ug_send[chunk * slots + k] = part.astype(BF16)
 
     def own_term(chunk):
-        return jnp.dot(w_ref[chunk, 0], ucat[chunk], preferred_element_type=F32)
+        hit = row == ids_of(chunk) - homes[0] * per
+        w = jnp.exp(logit_ref[chunk] - lse_ref[chunk]) - jnp.where(hit, 1.0, 0.0)
+        return jnp.dot(w.astype(BF16), ucat[chunk], preferred_element_type=F32)
 
     def mate_term(k, chunk):
         hit = row == lane_ids(mate_ids.at[k], chunk) - homes[0] * per
@@ -337,12 +362,33 @@
     for copy in (lse_copies[1], lse_copies[2], lse_copies[0]):
         copy.start()
     over_chunks(user_terms)
-    steps(half, 0, lambda step: far_copy(step, me).start())
-    steps(half, 1, lambda step: near_copy(step, me).start())
+    def low_first(body):
+        if peers <= 8:
+            for peer in range(peers):
+                body(peer)
+        else:
+            pl.loop(0, peers)(body)
+
+    def give(peer):
+        @pl.when(peer // half != side)
+        def _():
+            to_far(peer, me).start()
+
+        @pl.when(jnp.logical_and(peer // half == side, peer != me))
+        def _():
+            to_near(peer, me).start()
+
+    low_first(give)
     ig_ref[...] = total_of(own_term)
     for p in range(2):
         mate_in(2, p)
     over_chunks(functools.partial(meet, 2))
+    each(lambda step: stat_copy(step, me).wait_send())
+    for p in range(2):
+        for copy in (*to_mates[0][p], *to_mates[1][p], *onward[p]):
+            copy.wait_send()
+    for copy in lse_copies:
+        copy.wait_send()
     for k in range(3):
         lse_copies[k].wait_recv()
         ig_ref[...] += total_of(functools.partial(mate_term, k))
@@ -365,15 +411,6 @@
 
     steps(half, 1, gather_near)
     steps(half, 0, gather_far)
-    for copy in from_other + from_twin + from_diag:
-        copy.wait_send()
-    for p in range(2):
-        for copy in (*to_mates[0][p], *to_mates[1][p], *onward[p]):
-            copy.wait_send()
-    for copy in lse_copies:
-        copy.wait_send()
-    for copy in (users_copy, pos_copy, stat_copy):
-        each(lambda step: copy(step, me).wait_send())
     steps(half, 0, lambda step: far_copy(step, me).wait_send())
     steps(half, 1, lambda step: near_copy(step, me).wait_send())
 
@@ -413,8 +450,10 @@
             pltpu.VMEM((peers, 1, own), jnp.int32),
             pltpu.VMEM((QUAD, per, width), BF16),
             pltpu.VMEM((chunks, lanes, width), BF16),
-            pltpu.VMEM((chunks, QUAD, per, lanes), F32),
             pltpu.VMEM((chunks, QUAD, per, lanes), BF16),
+            pltpu.VMEM((chunks, per, lanes), F32),
+            pltpu.VMEM((chunks, lanes, width), F32),
+            pltpu.VMEM((chunks, lanes, width), F32),
             pltpu.VMEM((chunks, QUAD, 1, lanes), F32),
             pltpu.VMEM((chunks, QUAD, 2, lanes), F32),
             pltpu.VMEM((chunks, 1, lanes), F32),

time: 24.3 us -> 23.5 us (0.967)
  Pallas kernels: 23.5 us -> 22.7 us
    pallas_call x1, Pallas kernels: 22.7 us -> 22 us  [local(): pl.pallas_call(functools.partial(kernel, peers, slots), out_shape=(pltpu....]
where the time goes in v3:
time: 23.5 us; the launch traced here: 23.3 us
  Pallas kernels  22.7 us (97%)
  between operations  0.64 us (3%)
    pallas_call x1, Pallas kernels, local(): pl.pallas_call(functools.partial(kernel, peers, slots), out_shape=(pltpu....  22 us
    pallas_call x1, Pallas kernels, local(): pl.pallas_call(settle, out_shape=(jax.ShapeDtypeStruct((1, own), F32), ja...  0.73 us

profile of v3, /device:TPU:0, one launch (start us, length us, event | category | flops | bytes accessed | tf_op | source)
XLA Modules:
  0.0 23.3 jit_solution(2842181237194704521)
XLA Ops:
  0.6 22.0 %shard_map.58 = (f32[1,40]{1,0:T(1,128)S(1)}, f32[40,256]{1,0:T(8,128)S(1)}, f32[256,256]{1,0:T(8,128)S(1)}) custom-call(bf16[40,256]{1,0:T(8,128)(2,1)} %users_ref.1, bf16[256,256]{1,0:T(8,128)(2,1)} %items_ref.1, s32[1,40]{1,0:T(1,128)} %bitcast.2), custom_call_target="tpu_custom_call" | custom-call | tf_op jit(solution)/shard_map/pallas_call | solution.py:439
  22.6 0.7 %shard_map.59 = (f32[1,40]{1,0:T(1,128)}, f32[40,256]{1,0:T(8,128)}, f32[256,256]{1,0:T(8,128)}) custom-call(f32[1,40]{1,0:T(1,128)S(1)} %get-tuple-element.9.loss_in, f32[40,256]{1,0:T(8,128)S(1)} %get-tuple-element.10.ug_in, f32[256,256]{1,0:T(8,128)S(1)} %get-tuple-element.11.ig_in), custom_call_target="tpu_custom_call" | custom-call | tf_op jit(solution)/shard_map/pallas_call | solution.py:488

commit v4 on v3

--- a/solution.py
+++ b/solution.py
@@ -20,9 +20,9 @@
 def kernel(
     peers, slots, users_ref, items_ref, pos_ref,
     loss_ref, ug_ref, ig_ref,
-    uall, pall, iall, ucat, e_ref, logit_ref, blend, picked, top_ref, part_ref, loss_all, stat, stat_all,
+    uall, pall, iall, ucat, e_ref, logit_ref, blend, picked, total_ref, stat, stat_all, pos, pos_all,
     term, ug_send, near_recv, far_recv, mates, mate_ids, mate_cat, mate_logit, lse_ref, mate_lse,
-    u_ss, u_rs, p_ss, p_rs, i_ss, i_rs, s_ss, s_rs, g_ss, g_rs, m_ss, m_rs, n_ss, n_rs, l_ss, l_rs,
+    u_ss, u_rs, p_ss, p_rs, i_ss, i_rs, s_ss, s_rs, h_ss, h_rs, g_ss, g_rs, m_ss, m_rs, n_ss, n_rs, l_ss, l_rs,
     in_sem, ready, x_ready,
 ):
     own = users_ref.shape[0]
@@ -216,14 +216,20 @@
 
     steps(half, 1, near_in)
     lend(0)
-    steps(half, 0, far_in)
-    lend(1)
 
     def over_chunks(body):
-        if chunks == 1:
-            body(0)
+        if chunks <= 2:
+            for chunk in range(chunks):
+                body(chunk)
         else:
             pl.loop(0, chunks)(body)
+
+    def over_half(which, body):
+        count = chunks // 2
+        if count == 1:
+            body(which)
+        else:
+            pl.loop(0, count)(lambda chunk: body(which * count + chunk))
 
     homes = (
         batch * total_index + index,
@@ -253,37 +259,30 @@
             iall[0], mate_cat[k, chunk], NT, preferred_element_type=F32
         )
 
-    def forward(q, chunk):
-        logit = lax.dot_general(iall[q], ucat[chunk], NT, preferred_element_type=F32)
+    def forward(chunk):
+        items = iall[...].reshape(QUAD * per, iall.shape[2])
+        logit = lax.dot_general(items, ucat[chunk], NT, preferred_element_type=F32)
         top = jnp.max(logit, axis=0, keepdims=True)
-        hit = row == ids_of(chunk) - homes[q] * per
         e = jnp.exp(logit - top)
-        e_ref[chunk, q] = e.astype(BF16)
-        if q == 0:
-            logit_ref[chunk] = logit
-        top_ref[chunk, q] = top
-        part_ref[chunk, q, 0:1] = jnp.sum(e, axis=0, keepdims=True)
-        part_ref[chunk, q, 1:2] = jnp.sum(jnp.where(hit, logit, 0.0), axis=0, keepdims=True)
-
-    def summarize(chunk):
-        tops = top_ref[chunk]
-        top = jnp.max(tops, axis=0)
-        total = jnp.sum(part_ref[chunk, :, 0:1] * jnp.exp(tops - top[None]), axis=0)
-        stat[chunk, 0:1] = top + jnp.log(total)
-        stat[chunk, 1:2] = jnp.sum(part_ref[chunk, :, 1:2], axis=0)
-
-    over_chunks(prepare)
-    over_chunks(functools.partial(forward, 0))
-    for copy in from_twin:
+        total = jnp.sum(e, axis=0, keepdims=True)
+        stat[chunk] = top + jnp.log(total)
+        total_ref[chunk] = total
+        e_ref[chunk] = e.astype(BF16)
+        logit_ref[chunk] = logit[:per]
+
+    for copy in from_twin + from_diag:
         copy.wait_recv()
-    over_chunks(functools.partial(forward, 1))
-    over_chunks(functools.partial(forward, 2))
-    for copy in from_diag:
-        copy.wait_recv()
-    over_chunks(functools.partial(forward, 3))
-    over_chunks(summarize)
+
+    def advance(chunk):
+        prepare(chunk)
+        forward(chunk)
+
+    over_half(side, advance)
+    steps(half, 0, far_in)
+    over_half(1 - side, advance)
     each(lambda step: stat_copy(step, me).start())
     stat_all[me] = stat[...]
+    lend(1)
 
     def mate_in(k, p):
         for copy in mate_copy(uall, pall, k, p, halves[p], to_twin):
@@ -293,28 +292,35 @@
         return jnp.transpose(jnp.concatenate([rows] * (8 // rows.shape[0]), axis=0))
 
     def gather_terms(chunk):
-        share = columns(
-            jnp.concatenate([top_ref[chunk, q] - stat[chunk, 0:1] for q in range(QUAD)], axis=0)
-        )
+        share = 1.0 / columns(total_ref[chunk])[:, 0:1]
         mix = jnp.zeros((slots * own, ucat.shape[2]), F32)
         pick = jnp.zeros((slots * own, ucat.shape[2]), F32)
         for q in range(QUAD):
-            hit = jnp.where(row == ids_of(chunk) - homes[q] * per, 1.0, 0.0).astype(BF16)
-            part = lax.dot_general(e_ref[chunk, q], iall[q], TN, preferred_element_type=F32)
-            mix = mix + part * jnp.exp(share[:, q : q + 1])
+            here = row == ids_of(chunk) - homes[q] * per
+            hit = jnp.where(here, 1.0, 0.0).astype(BF16)
+            rest = jnp.where(here, 0.0, e_ref[chunk, q * per : (q + 1) * per].astype(F32)).astype(BF16)
+            part = lax.dot_general(rest, iall[q], TN, preferred_element_type=F32)
+            mix = mix + part
             pick = pick + lax.dot_general(hit, iall[q], TN, preferred_element_type=F32)
-        blend[chunk] = mix
+        blend[chunk] = mix * share
         picked[chunk] = pick
+        pos[chunk] = lax.dot_general(
+            jnp.ones((8, pick.shape[1]), F32), ucat[chunk].astype(F32) * pick, NT,
+            precision=lax.Precision.HIGHEST, preferred_element_type=F32,
+        )[0:1]
+
+    def pos_out(step, source):
+        return remote(pos, pos_all.at[source], h_ss.at[step], h_rs.at[source], at(peer_at(step)))
 
     over_chunks(gather_terms)
+    each(lambda step: pos_out(step, me).start())
+    pos_all[me] = pos[...]
     for p in range(2):
         mate_in(0, p)
     over_chunks(functools.partial(meet, 0))
-    for p in range(2):
-        mate_in(1, p)
-        for copy in onward[p]:
-            copy.start()
-    over_chunks(functools.partial(meet, 1))
+    mate_in(1, 0)
+    for copy in onward[0]:
+        copy.start()
     for copy in from_other + from_twin + from_diag:
         copy.wait_send()
     for copy in (users_copy, pos_copy):
@@ -323,16 +329,17 @@
 
 
     def rescale(chunk):
-        parts = stat_all[:, chunk]
-        lses = parts[:, 0:1]
+        lses = stat_all[:, chunk]
         peak = jnp.max(lses, axis=0)
-        lse = peak + jnp.log(jnp.sum(jnp.exp(lses - peak[None]), axis=0))
-        lse_ref[chunk] = lse
-        loss_all[chunk] = lse - jnp.sum(parts[:, 1:2], axis=0)
+        lse_ref[chunk] = peak + jnp.log(jnp.sum(jnp.exp(lses - peak[None]), axis=0))
 
     def user_terms(chunk):
-        share = columns(stat[chunk, 0:1] - lse_ref[chunk])[:, 0:1]
-        grad = blend[chunk] * jnp.exp(share) - picked[chunk]
+        lse = lse_ref[chunk]
+        at_pos = jnp.exp(jnp.minimum(pos[chunk] - lse, 0.0)) - 1.0
+        scale = columns(
+            jnp.concatenate([jnp.exp(stat[chunk] - lse), at_pos.astype(BF16).astype(F32)], axis=0)
+        )
+        grad = blend[chunk] * scale[:, 0:1] + picked[chunk] * scale[:, 1:2]
         for k in range(slots):
             part = grad[k * own : (k + 1) * own]
             term[chunk * slots + k] = part
@@ -349,8 +356,8 @@
         return jnp.dot(w.astype(BF16), mate_cat[k, chunk], preferred_element_type=F32)
 
     def total_of(one):
-        if chunks == 1:
-            return one(0)
+        if chunks == 2:
+            return one(0) + one(1)
         return lax.fori_loop(1, chunks, lambda chunk, acc: acc + one(chunk), one(0))
 
     lse_copies = [
@@ -380,20 +387,26 @@
 
     low_first(give)
     ig_ref[...] = total_of(own_term)
+    mate_in(1, 1)
+    for copy in onward[1]:
+        copy.start()
+    over_chunks(functools.partial(meet, 1))
     for p in range(2):
         mate_in(2, p)
     over_chunks(functools.partial(meet, 2))
     each(lambda step: stat_copy(step, me).wait_send())
+    each(lambda step: pos_out(step, me).wait_send())
     for p in range(2):
         for copy in (*to_mates[0][p], *to_mates[1][p], *onward[p]):
             copy.wait_send()
     for copy in lse_copies:
         copy.wait_send()
-    for k in range(3):
+    for k in (0, 2, 1):
         lse_copies[k].wait_recv()
         ig_ref[...] += total_of(functools.partial(mate_term, k))
 
-    losses = loss_all[me // slots]
+    each(lambda step: pos_out(step, peer_at(step)).wait_recv())
+    losses = lse_ref[me // slots] - jnp.sum(pos_all[:, me // slots], axis=0)
     loss = jnp.zeros((1, own), F32)
     for k in range(slots):
         loss = jnp.where(lax.rem(me, slots) == k, losses[:, k * own : (k + 1) * own], loss)
@@ -430,7 +443,7 @@
     own, width = users.shape
     per = items.shape[0]
     peers = lax.axis_size("items") // 2
-    slots = math.gcd(peers, 8)
+    slots = math.gcd(peers // 2, 4)
     chunks = peers // slots
     lanes = slots * own
     dma = pltpu.SemaphoreType.DMA
@@ -450,15 +463,15 @@
             pltpu.VMEM((peers, 1, own), jnp.int32),
             pltpu.VMEM((QUAD, per, width), BF16),
             pltpu.VMEM((chunks, lanes, width), BF16),
-            pltpu.VMEM((chunks, QUAD, per, lanes), BF16),
+            pltpu.VMEM((chunks, QUAD * per, lanes), BF16),
             pltpu.VMEM((chunks, per, lanes), F32),
             pltpu.VMEM((chunks, lanes, width), F32),
             pltpu.VMEM((chunks, lanes, width), F32),
-            pltpu.VMEM((chunks, QUAD, 1, lanes), F32),
-            pltpu.VMEM((chunks, QUAD, 2, lanes), F32),
             pltpu.VMEM((chunks, 1, lanes), F32),
-            pltpu.VMEM((chunks, 2, lanes), F32),
-            pltpu.VMEM((peers, chunks, 2, lanes), F32),
+            pltpu.VMEM((chunks, 1, lanes), F32),
+            pltpu.VMEM((peers, chunks, 1, lanes), F32),
+            pltpu.VMEM((chunks, 1, lanes), F32),
+            pltpu.VMEM((peers, chunks, 1, lanes), F32),
             pltpu.VMEM((peers, own, width), F32),
             pltpu.VMEM((peers, own, width), BF16),
             pltpu.VMEM((peers, own, width), F32),
@@ -474,6 +487,7 @@
             dma((QUAD, PARTS)), dma((QUAD, PARTS)),
             dma((peers,)), dma((peers,)),
             dma((peers,)), dma((peers,)),
+            dma((peers,)), dma((peers,)),
             dma((3, 2)), dma((3, 2)),
             dma((3, 2)), dma((3, 2)),
             dma((3,)), dma((3,)),
@@ -482,7 +496,7 @@
             pltpu.SemaphoreType.REGULAR((1,)),
         ],
         compiler_params=pltpu.CompilerParams(
-            collective_id=0, has_side_effects=True, vmem_limit_bytes=48 * 1024 * 1024
+            collective_id=0, has_side_effects=True, vmem_limit_bytes=56 * 1024 * 1024
         ),
     )(*(pltpu.with_memory_space_constraint(v, pltpu.HBM) for v in (users, items, pos_ids.reshape(1, own))))
     loss, user_grad, item_grad = pl.pallas_call(

time: 23.5 us -> 23.2 us (0.987)
  Pallas kernels: 22.7 us -> 22.4 us
    pallas_call x1, Pallas kernels: 22 us -> 21.7 us  [local(): pl.pallas_call(functools.partial(kernel, peers, slots), out_shape=(pltpu....]
where the time goes in v4:
time: 23.2 us; the launch traced here: 23 us
  Pallas kernels  22.4 us (97%)
  between operations  0.64 us (3%)
    pallas_call x1, Pallas kernels, local(): pl.pallas_call(functools.partial(kernel, peers, slots), out_shape=(pltpu....  21.7 us
    pallas_call x1, Pallas kernels, local(): pl.pallas_call(settle, out_shape=(jax.ShapeDtypeStruct((1, own), F32), ja...  0.73 us

profile of v4, /device:TPU:0, one launch (start us, length us, event | category | flops | bytes accessed | tf_op | source)
XLA Modules:
  0.0 23.0 jit_solution(17131422713388031786)
XLA Ops:
  0.6 21.7 %shard_map.58 = (f32[1,40]{1,0:T(1,128)S(1)}, f32[40,256]{1,0:T(8,128)S(1)}, f32[256,256]{1,0:T(8,128)S(1)}) custom-call(bf16[40,256]{1,0:T(8,128)(2,1)} %users_ref.1, bf16[256,256]{1,0:T(8,128)(2,1)} %items_ref.1, s32[1,40]{1,0:T(1,128)} %bitcast.2), custom_call_target="tpu_custom_call" | custom-call | tf_op jit(solution)/shard_map/pallas_call | solution.py:452
  22.3 0.7 %shard_map.59 = (f32[1,40]{1,0:T(1,128)}, f32[40,256]{1,0:T(8,128)}, f32[256,256]{1,0:T(8,128)}) custom-call(f32[1,40]{1,0:T(1,128)S(1)} %get-tuple-element.9.loss_in, f32[40,256]{1,0:T(8,128)S(1)} %get-tuple-element.10.ug_in, f32[256,256]{1,0:T(8,128)S(1)} %get-tuple-element.11.ig_in), custom_call_target="tpu_custom_call" | custom-call | tf_op jit(solution)/shard_map/pallas_call | solution.py:502

commit v5 on v4

--- a/solution.py
+++ b/solution.py
@@ -20,7 +20,7 @@
 def kernel(
     peers, slots, users_ref, items_ref, pos_ref,
     loss_ref, ug_ref, ig_ref,
-    uall, pall, iall, ucat, e_ref, logit_ref, blend, picked, total_ref, stat, stat_all, pos, pos_all,
+    uall, pall, iall, ucat, e_ref, logit_ref, blend, picked, top_ref, stat, stat_all, pos, pos_all,
     term, ug_send, near_recv, far_recv, mates, mate_ids, mate_cat, mate_logit, lse_ref, mate_lse,
     u_ss, u_rs, p_ss, p_rs, i_ss, i_rs, s_ss, s_rs, h_ss, h_rs, g_ss, g_rs, m_ss, m_rs, n_ss, n_rs, l_ss, l_rs,
     in_sem, ready, x_ready,
@@ -151,8 +151,17 @@
     from_twin = [items_copy(0, 1, p, to_twin) for p in range(PARTS)]
     from_diag = [items_copy(2, 3, p, to_twin) for p in range(PARTS)]
 
-    def send_down(step):
-        @pl.when(peer_at(step) < me)
+    def low_first(body):
+        if peers <= 8:
+            for peer in range(peers):
+                body(peer)
+        else:
+            pl.loop(0, peers)(body)
+
+    def send_down(peer):
+        step = lax.rem(peer - me + peers, peers)
+
+        @pl.when(peer < me)
         def _():
             pos_copy(step, me).start()
             users_copy(step, me).start()
@@ -171,7 +180,7 @@
         for copy in from_other:
             copy.start()
 
-    each(send_down)
+    low_first(send_down)
     for copy in from_twin:
         copy.start()
 
@@ -259,16 +268,24 @@
             iall[0], mate_cat[k, chunk], NT, preferred_element_type=F32
         )
 
+    def folded(combine, block):
+        return combine(block.reshape(block.shape[0] // 8, 8, block.shape[1]), axis=0)
+
     def forward(chunk):
-        items = iall[...].reshape(QUAD * per, iall.shape[2])
-        logit = lax.dot_general(items, ucat[chunk], NT, preferred_element_type=F32)
-        top = jnp.max(logit, axis=0, keepdims=True)
-        e = jnp.exp(logit - top)
-        total = jnp.sum(e, axis=0, keepdims=True)
-        stat[chunk] = top + jnp.log(total)
-        total_ref[chunk] = total
-        e_ref[chunk] = e.astype(BF16)
-        logit_ref[chunk] = logit[:per]
+        logits = [
+            lax.dot_general(iall[q], ucat[chunk], NT, preferred_element_type=F32)
+            for q in range(QUAD)
+        ]
+        tops = [folded(jnp.max, logit) for logit in logits]
+        top = jnp.max(functools.reduce(jnp.maximum, tops), axis=0, keepdims=True)
+        total = jnp.zeros_like(tops[0])
+        for q in range(QUAD):
+            e = jnp.exp(logits[q] - top)
+            e_ref[chunk, q * per : (q + 1) * per] = e.astype(BF16)
+            total = total + folded(jnp.sum, e)
+        stat[chunk] = top + jnp.log(jnp.sum(total, axis=0, keepdims=True))
+        top_ref[chunk] = top
+        logit_ref[chunk] = logits[0]
 
     for copy in from_twin + from_diag:
         copy.wait_recv()
@@ -280,7 +297,12 @@
     over_half(side, advance)
     steps(half, 0, far_in)
     over_half(1 - side, advance)
-    each(lambda step: stat_copy(step, me).start())
+    def tell(peer):
+        @pl.when(peer != me)
+        def _():
+            stat_copy(lax.rem(peer - me + peers, peers), me).start()
+
+    low_first(tell)
     stat_all[me] = stat[...]
     lend(1)
 
@@ -292,7 +314,6 @@
         return jnp.transpose(jnp.concatenate([rows] * (8 // rows.shape[0]), axis=0))
 
     def gather_terms(chunk):
-        share = 1.0 / columns(total_ref[chunk])[:, 0:1]
         mix = jnp.zeros((slots * own, ucat.shape[2]), F32)
         pick = jnp.zeros((slots * own, ucat.shape[2]), F32)
         for q in range(QUAD):
@@ -302,7 +323,7 @@
             part = lax.dot_general(rest, iall[q], TN, preferred_element_type=F32)
             mix = mix + part
             pick = pick + lax.dot_general(hit, iall[q], TN, preferred_element_type=F32)
-        blend[chunk] = mix * share
+        blend[chunk] = mix
         picked[chunk] = pick
         pos[chunk] = lax.dot_general(
             jnp.ones((8, pick.shape[1]), F32), ucat[chunk].astype(F32) * pick, NT,
@@ -336,9 +357,8 @@
     def user_terms(chunk):
         lse = lse_ref[chunk]
         at_pos = jnp.exp(jnp.minimum(pos[chunk] - lse, 0.0)) - 1.0
-        scale = columns(
-            jnp.concatenate([jnp.exp(stat[chunk] - lse), at_pos.astype(BF16).astype(F32)], axis=0)
-        )
+        at_top = jnp.exp(top_ref[chunk] - lse)
+        scale = columns(jnp.concatenate([at_top, at_pos], axis=0).astype(BF16).astype(F32))
         grad = blend[chunk] * scale[:, 0:1] + picked[chunk] * scale[:, 1:2]
         for k in range(slots):
             part = grad[k * own : (k + 1) * own]
@@ -369,13 +389,6 @@
     for copy in (lse_copies[1], lse_copies[2], lse_copies[0]):
         copy.start()
     over_chunks(user_terms)
-    def low_first(body):
-        if peers <= 8:
-            for peer in range(peers):
-                body(peer)
-        else:
-            pl.loop(0, peers)(body)
-
     def give(peer):
         @pl.when(peer // half != side)
         def _():

time: 23.2 us -> 23 us (level)
  no operation moved by 1% of the time
where the time goes in v5:
time: 23 us; the launch traced here: 22.8 us
  Pallas kernels  22.2 us (97%)
  between operations  0.64 us (3%)
    pallas_call x1, Pallas kernels, local(): pl.pallas_call(functools.partial(kernel, peers, slots), out_shape=(pltpu....  21.4 us
    pallas_call x1, Pallas kernels, local(): pl.pallas_call(settle, out_shape=(jax.ShapeDtypeStruct((1, own), F32), ja...  0.73 us

profile of v5, /device:TPU:0, one launch (start us, length us, event | category | flops | bytes accessed | tf_op | source)
XLA Modules:
  0.0 22.8 jit_solution(4853769885742253437)
XLA Ops:
  0.6 21.4 %shard_map.58 = (f32[1,40]{1,0:T(1,128)S(1)}, f32[40,256]{1,0:T(8,128)S(1)}, f32[256,256]{1,0:T(8,128)S(1)}) custom-call(bf16[40,256]{1,0:T(8,128)(2,1)} %users_ref.1, bf16[256,256]{1,0:T(8,128)(2,1)} %items_ref.1, s32[1,40]{1,0:T(1,128)} %bitcast.2), custom_call_target="tpu_custom_call" | custom-call | tf_op jit(solution)/shard_map/pallas_call | solution.py:465
  22.1 0.7 %shard_map.59 = (f32[1,40]{1,0:T(1,128)}, f32[40,256]{1,0:T(8,128)}, f32[256,256]{1,0:T(8,128)}) custom-call(f32[1,40]{1,0:T(1,128)S(1)} %get-tuple-element.9.loss_in, f32[40,256]{1,0:T(8,128)S(1)} %get-tuple-element.10.ug_in, f32[256,256]{1,0:T(8,128)S(1)} %get-tuple-element.11.ig_in), custom_call_target="tpu_custom_call" | custom-call | tf_op jit(solution)/shard_map/pallas_call | solution.py:515

commit v6 on v5

--- a/solution.py
+++ b/solution.py
@@ -163,8 +163,8 @@
 
         @pl.when(peer < me)
         def _():
+            users_copy(step, me).start()
             pos_copy(step, me).start()
-            users_copy(step, me).start()
 
     def send_up(step):
         peer = peer_at(step)
@@ -172,8 +172,8 @@
         @pl.when(peer > me)
         def _():
             pl.semaphore_wait(ready.at[peer], 1)
+            users_copy(step, me).start()
             pos_copy(step, me).start()
-            users_copy(step, me).start()
 
     @pl.when(batch == 1)
     def _():
@@ -197,31 +197,31 @@
     def near_in(step):
         source = near_at(step)
         users_copy(step, source).wait_recv()
-        pos_copy(step, source).wait_recv()
 
     def far_in(step):
         source = far_at(step)
         users_copy(step, source).wait_recv()
-        pos_copy(step, source).wait_recv()
-
-    def mate_copy(src, ids, k, p, part, device):
+
+    def mate_copy(src, k, p, part, device):
         block = pl.ds(part * half, half)
-        return (
-            remote(ids.at[block], mate_ids.at[k, block], n_ss.at[k, p], n_rs.at[k, p], device),
-            remote(src.at[block], mates.at[k, block], m_ss.at[k, p], m_rs.at[k, p], device),
-        )
+        return remote(src.at[block], mates.at[k, block], m_ss.at[k, p], m_rs.at[k, p], device)
+
+    def ids_copy(src, k, device):
+        return remote(src, mate_ids.at[k], n_ss.at[k], n_rs.at[k], device)
+
+    ids_to_mates = (ids_copy(pall, 1, to_other), ids_copy(pall, 0, to_twin))
+    ids_onward = ids_copy(mate_ids.at[1], 2, to_twin)
 
     halves = (side, 1 - side)
     to_mates = [
-        [mate_copy(uall, pall, 1, p, halves[p], to_other) for p in range(2)],
-        [mate_copy(uall, pall, 0, p, halves[p], to_twin) for p in range(2)],
+        [mate_copy(uall, 1, p, halves[p], to_other) for p in range(2)],
+        [mate_copy(uall, 0, p, halves[p], to_twin) for p in range(2)],
     ]
-    onward = [mate_copy(mates.at[1], mate_ids.at[1], 2, p, halves[p], to_twin) for p in range(2)]
+    onward = [mate_copy(mates.at[1], 2, p, halves[p], to_twin) for p in range(2)]
 
     def lend(p):
         for pair in to_mates:
-            for copy in pair[p]:
-                copy.start()
+            pair[p].start()
 
     steps(half, 1, near_in)
     lend(0)
@@ -305,10 +305,12 @@
     low_first(tell)
     stat_all[me] = stat[...]
     lend(1)
+    each(lambda step: pos_copy(step, peer_at(step)).wait_recv())
+    for copy in ids_to_mates:
+        copy.start()
 
     def mate_in(k, p):
-        for copy in mate_copy(uall, pall, k, p, halves[p], to_twin):
-            copy.wait_recv()
+        mate_copy(uall, k, p, halves[p], to_twin).wait_recv()
 
     def columns(rows):
         return jnp.transpose(jnp.concatenate([rows] * (8 // rows.shape[0]), axis=0))
@@ -340,8 +342,7 @@
         mate_in(0, p)
     over_chunks(functools.partial(meet, 0))
     mate_in(1, 0)
-    for copy in onward[0]:
-        copy.start()
+    onward[0].start()
     for copy in from_other + from_twin + from_diag:
         copy.wait_send()
     for copy in (users_copy, pos_copy):
@@ -385,10 +386,6 @@
         for k, device in enumerate((to_twin, to_other, to_diag))
     ]
 
-    over_chunks(rescale)
-    for copy in (lse_copies[1], lse_copies[2], lse_copies[0]):
-        copy.start()
-    over_chunks(user_terms)
     def give(peer):
         @pl.when(peer // half != side)
         def _():
@@ -398,11 +395,35 @@
         def _():
             to_near(peer, me).start()
 
-    low_first(give)
+    def send_terms(chunk):
+        user_terms(chunk)
+        if chunks <= 2:
+            for k in range(slots):
+                give(chunk * slots + k)
+        else:
+            pl.loop(0, slots)(lambda k: give(chunk * slots + k))
+
+    def send_lses():
+        for copy in (lse_copies[1], lse_copies[2], lse_copies[0]):
+            copy.start()
+
+    if chunks <= 2:
+        rescale(0)
+        send_terms(0)
+        for chunk in range(1, chunks):
+            rescale(chunk)
+        send_lses()
+        for chunk in range(1, chunks):
+            send_terms(chunk)
+    else:
+        over_chunks(rescale)
+        send_lses()
+        over_chunks(send_terms)
     ig_ref[...] = total_of(own_term)
     mate_in(1, 1)
-    for copy in onward[1]:
-        copy.start()
+    onward[1].start()
+    ids_to_mates[0].wait_recv()
+    ids_onward.start()
     over_chunks(functools.partial(meet, 1))
     for p in range(2):
         mate_in(2, p)
@@ -410,8 +431,12 @@
     each(lambda step: stat_copy(step, me).wait_send())
     each(lambda step: pos_out(step, me).wait_send())
     for p in range(2):
-        for copy in (*to_mates[0][p], *to_mates[1][p], *onward[p]):
+        for copy in (to_mates[0][p], to_mates[1][p], onward[p]):
             copy.wait_send()
+    for copy in (*ids_to_mates, ids_onward):
+        copy.wait_send()
+    ids_to_mates[1].wait_recv()
+    ids_onward.wait_recv()
     for copy in lse_copies:
         copy.wait_send()
     for k in (0, 2, 1):
@@ -435,10 +460,10 @@
         far_copy(step, far_at(step)).wait_recv()
         ug_ref[...] += far_recv[far_at(step)].astype(F32)
 
+    steps(half, 0, lambda step: far_copy(step, me).wait_send())
+    steps(half, 1, lambda step: near_copy(step, me).wait_send())
     steps(half, 1, gather_near)
     steps(half, 0, gather_far)
-    steps(half, 0, lambda step: far_copy(step, me).wait_send())
-    steps(half, 1, lambda step: near_copy(step, me).wait_send())
 
 
 def settle(loss_in, ug_in, ig_in, loss_out, ug_out, ig_out, sems):
@@ -502,7 +527,7 @@
             dma((peers,)), dma((peers,)),
             dma((peers,)), dma((peers,)),
             dma((3, 2)), dma((3, 2)),
-            dma((3, 2)), dma((3, 2)),
+            dma((3,)), dma((3,)),
             dma((3,)), dma((3,)),
             dma((3,)),
             pltpu.SemaphoreType.REGULAR((peers,)),

time: 23 us -> 22.8 us (level)
  no operation moved by 1% of the time
where the time goes in v6:
time: 22.8 us; the launch traced here: 22.7 us
  Pallas kernels  22.1 us (97%)
  between operations  0.64 us (3%)
    pallas_call x1, Pallas kernels, local(): pl.pallas_call(functools.partial(kernel, peers, slots), out_shape=(pltpu....  21.3 us
    pallas_call x1, Pallas kernels, local(): pl.pallas_call(settle, out_shape=(jax.ShapeDtypeStruct((1, own), F32), ja...  0.73 us

profile of v6, /device:TPU:0, one launch (start us, length us, event | category | flops | bytes accessed | tf_op | source)
XLA Modules:
  0.0 22.7 jit_solution(17876850958770516169)
XLA Ops:
  0.6 21.3 %shard_map.58 = (f32[1,40]{1,0:T(1,128)S(1)}, f32[40,256]{1,0:T(8,128)S(1)}, f32[256,256]{1,0:T(8,128)S(1)}) custom-call(bf16[40,256]{1,0:T(8,128)(2,1)} %users_ref.1, bf16[256,256]{1,0:T(8,128)(2,1)} %items_ref.1, s32[1,40]{1,0:T(1,128)} %bitcast.2), custom_call_target="tpu_custom_call" | custom-call | tf_op jit(solution)/shard_map/pallas_call | solution.py:490
  22.0 0.7 %shard_map.59 = (f32[1,40]{1,0:T(1,128)}, f32[40,256]{1,0:T(8,128)}, f32[256,256]{1,0:T(8,128)}) custom-call(f32[1,40]{1,0:T(1,128)S(1)} %get-tuple-element.9.loss_in, f32[40,256]{1,0:T(8,128)S(1)} %get-tuple-element.10.ug_in, f32[256,256]{1,0:T(8,128)S(1)} %get-tuple-element.11.ig_in), custom_call_target="tpu_custom_call" | custom-call | tf_op jit(solution)/shard_map/pallas_call | solution.py:540

commit v7 on v6

--- a/solution.py
+++ b/solution.py
@@ -70,6 +70,13 @@
         else:
             pl.loop(1, peers)(body)
 
+    def low_first(body):
+        if peers <= 8:
+            for peer in range(peers):
+                body(peer)
+        else:
+            pl.loop(0, peers)(body)
+
     def greet(step):
         peer = peer_at(step)
 
@@ -77,9 +84,7 @@
         def _():
             pl.semaphore_signal(barrier, inc=1, device_id=at(peer), device_id_type=MESH)
 
-    def answer(step):
-        peer = peer_at(step)
-
+    def answer(peer):
         @pl.when(peer < me)
         def _():
             pl.semaphore_signal(ready.at[me], inc=1, device_id=at(peer), device_id_type=MESH)
@@ -99,11 +104,11 @@
     for copy in mine_in:
         copy.start()
     pl.semaphore_wait(barrier, me + batch + 1)
-    each(answer)
-
     @pl.when(batch == 1)
     def _():
         pl.semaphore_signal(x_ready.at[0], inc=1, device_id=to_other, device_id_type=MESH)
+
+    low_first(answer)
 
     for copy in mine_in:
         copy.wait()
@@ -150,13 +155,6 @@
     from_other = [items_copy(0, 2, p, to_other) for p in range(PARTS)]
     from_twin = [items_copy(0, 1, p, to_twin) for p in range(PARTS)]
     from_diag = [items_copy(2, 3, p, to_twin) for p in range(PARTS)]
-
-    def low_first(body):
-        if peers <= 8:
-            for peer in range(peers):
-                body(peer)
-        else:
-            pl.loop(0, peers)(body)
 
     def send_down(peer):
         step = lax.rem(peer - me + peers, peers)

time: 22.8 us -> 22.8 us (level)
  no operation moved by 1% of the time
where the time goes in v7:
time: 22.8 us; the launch traced here: 22.7 us
  Pallas kernels  22.1 us (97%)
  between operations  0.64 us (3%)
    pallas_call x1, Pallas kernels, local(): pl.pallas_call(functools.partial(kernel, peers, slots), out_shape=(pltpu....  21.3 us
    pallas_call x1, Pallas kernels, local(): pl.pallas_call(settle, out_shape=(jax.ShapeDtypeStruct((1, own), F32), ja...  0.73 us

profile of v7, /device:TPU:0, one launch (start us, length us, event | category | flops | bytes accessed | tf_op | source)
XLA Modules:
  0.0 22.7 jit_solution(17624068340257180023)
XLA Ops:
  0.6 21.3 %shard_map.58 = (f32[1,40]{1,0:T(1,128)S(1)}, f32[40,256]{1,0:T(8,128)S(1)}, f32[256,256]{1,0:T(8,128)S(1)}) custom-call(bf16[40,256]{1,0:T(8,128)(2,1)} %users_ref.1, bf16[256,256]{1,0:T(8,128)(2,1)} %items_ref.1, s32[1,40]{1,0:T(1,128)} %bitcast.2), custom_call_target="tpu_custom_call" | custom-call | tf_op jit(solution)/shard_map/pallas_call | solution.py:488
  22.0 0.7 %shard_map.59 = (f32[1,40]{1,0:T(1,128)}, f32[40,256]{1,0:T(8,128)}, f32[256,256]{1,0:T(8,128)}) custom-call(f32[1,40]{1,0:T(1,128)S(1)} %get-tuple-element.9.loss_in, f32[40,256]{1,0:T(8,128)S(1)} %get-tuple-element.10.ug_in, f32[256,256]{1,0:T(8,128)S(1)} %get-tuple-element.11.ig_in), custom_call_target="tpu_custom_call" | custom-call | tf_op jit(solution)/shard_map/pallas_call | solution.py:538

commit v8 on v7

--- a/solution.py
+++ b/solution.py
@@ -14,7 +14,7 @@
 NT = (((1,), (1,)), ((), ()))
 TN = (((0,), (0,)), ((), ()))
 QUAD = 4
-PARTS = 2
+PARTS = 1
 
 
 def kernel(

time: 22.8 us -> 22.8 us (level)
  no operation moved by 1% of the time
where the time goes in v8:
time: 22.8 us; the launch traced here: 22.6 us
  Pallas kernels  22 us (96%)
  between operations  0.64 us (3%)
    pallas_call x1, Pallas kernels, local(): pl.pallas_call(functools.partial(kernel, peers, slots), out_shape=(pltpu....  21.3 us
    pallas_call x1, Pallas kernels, local(): pl.pallas_call(settle, out_shape=(jax.ShapeDtypeStruct((1, own), F32), ja...  0.73 us

profile of v8, /device:TPU:0, one launch (start us, length us, event | category | flops | bytes accessed | tf_op | source)
XLA Modules:
  0.0 22.6 jit_solution(11081105307340518770)
XLA Ops:
  0.6 21.3 %shard_map.58 = (f32[1,40]{1,0:T(1,128)S(1)}, f32[40,256]{1,0:T(8,128)S(1)}, f32[256,256]{1,0:T(8,128)S(1)}) custom-call(bf16[40,256]{1,0:T(8,128)(2,1)} %users_ref.1, bf16[256,256]{1,0:T(8,128)(2,1)} %items_ref.1, s32[1,40]{1,0:T(1,128)} %bitcast.2), custom_call_target="tpu_custom_call" | custom-call | tf_op jit(solution)/shard_map/pallas_call | solution.py:488
  21.9 0.7 %shard_map.59 = (f32[1,40]{1,0:T(1,128)}, f32[40,256]{1,0:T(8,128)}, f32[256,256]{1,0:T(8,128)}) custom-call(f32[1,40]{1,0:T(1,128)S(1)} %get-tuple-element.9.loss_in, f32[40,256]{1,0:T(8,128)S(1)} %get-tuple-element.10.ug_in, f32[256,256]{1,0:T(8,128)S(1)} %get-tuple-element.11.ig_in), custom_call_target="tpu_custom_call" | custom-call | tf_op jit(solution)/shard_map/pallas_call | solution.py:538
